TPU v7x, 32 devices: a whole 2x2x4 slice. The times are simulated.
32 devices in a mesh: col: 16 (over z, y, x), row: 2 (over core).
Axes of the slice: x: 2, y: 2, z: 4, core: 2. Of those that a mesh axis runs over, the one named last changes fastest.
Arguments:
- gradient: bfloat16 [4096, 16384], P('row', 'col'), may hold values from -120 to 120
- momentum: float32 [4096, 16384], P('row', 'col'), may hold values from -6 to 6
- right_factor: float32 [16384, 256], P(('col', 'row')), may hold values from -0.046875 to 0.046875
Outputs:
- momentum_next: float32 [4096, 16384], P('row', 'col')
- right_next: float32 [16384, 256], P(('col', 'row'))
- update: bfloat16 [4096, 16384], P('row', 'col')
All inputs are finite; a program needn't handle non-finite values.
Results may differ from a plain program's by a relative error of at most 0.0012.
Values sent between devices are 32-bit elements; how exact they have to be, the bound alone decides.
No kernel may reach another device: no remote copies, remote signals or barrier semaphores. Data moves between devices by JAX's collectives and lax.ppermute only.
A program may use at most 64 MiB of HBM per device.

v0:
```python
import math
import jax
import jax.numpy as jnp
from jax import lax
from jax.sharding import PartitionSpec as P

M = 4096
N = 16384
RANK = 256
EPS = 1e-06
FEEDBACK = 0.05


def body(gradient, momentum, right_factor):
    highest = lax.Precision.HIGHEST
    blend = momentum + gradient.astype(jnp.float32)
    right_block = lax.all_gather(right_factor, "row", axis=0, tiled=True)
    contract_rows = (((0,), (0,)), ((), ()))
    partial_value = jnp.dot(
        blend, right_block, precision=highest, preferred_element_type=jnp.float32
    )
    left = lax.psum(partial_value, "col")
    local_gram = lax.dot_general(
        left, left, contract_rows, precision=highest, preferred_element_type=jnp.float32
    )
    gram = lax.psum(local_gram, "row")
    lower = jnp.linalg.cholesky(gram)
    left_orth = jax.scipy.linalg.solve_triangular(lower, left.T, lower=True).T
    right_local = lax.dot_general(
        blend, left_orth, contract_rows, precision=highest, preferred_element_type=jnp.float32
    )
    share = lax.psum_scatter(right_local, "row", scatter_dimension=0, tiled=True)
    squares_right = lax.psum(jnp.sum(share * share, axis=0), ("col", "row"))
    right_norm = jnp.sqrt(squares_right + EPS)
    right_next = share / right_norm[None, :]
    right_whole = lax.all_gather(share, "row", axis=0, tiled=True)
    right_unit = right_whole / right_norm[None, :]
    contract_cols = (((1,), (1,)), ((), ()))
    feedback_term = lax.dot_general(
        left_orth, right_whole, contract_cols, precision=highest, preferred_element_type=jnp.float32
    )
    momentum_next = blend - FEEDBACK * feedback_term
    factor = math.sqrt(M * N / RANK)
    direction = lax.dot_general(
        left_orth, right_unit, contract_cols, precision=highest, preferred_element_type=jnp.float32
    )
    update = (factor * direction).astype(jnp.bfloat16)
    return (momentum_next, right_next, update)


def solution(mesh):
    placed = (P("row", "col"), P("row", "col"), P(("col", "row"), None))
    return jax.shard_map(
        body,
        mesh=mesh,
        in_specs=placed,
        out_specs=(P("row", "col"), P(("col", "row"), None), P("row", "col")),
        check_vma=False,
    )
```

profile of v0, /device:TPU:0, one launch (start us, length us, event | category | flops | bytes accessed | tf_op | source)
XLA Modules:
  0.0 361.9 jit_solution(6752334707807662119)
XLA Ops:
  7.2 0.7 all-gather.3.cloned.1.call-update
  7.9 13.4 %all-gather.3.cloned.1.call-done = f32[1024,256]{1,0:T(8,128)} async-done(((f32[512,256]{1,0:T(8,128)}), f32[1024,256]{1,0:T(8,128)}) %all-gather.3.cloned.1.call-update) | async-done | bytes 1048592 | tf_op jit(solution)/shard_map/all_gather | solution.py:17
  21.3 11.0 %fusion.1 = f32[2048,256]{1,0:T(8,128)} fusion(f32[1024,256]{1,0:T(8,128)} %all-gather.3.cloned.1.call-done, f32[2048,1024]{1,0:T(8,128)} %param.4, bf16[2048,1024]{1,0:T(8,128)(2,1)} %param.3), kind=kOutput, calls=%fused_computation.6 | convolution fusion | flops 6446645248 | bytes 15728640 | tf_op jit(solution)/shard_map/dot_general | solution.py:19
  32.3 127.9 %all-reduce.4.cloned.1.call-done = f32[2048,256]{1,0:T(8,128)} async-done(((f32[2048,256]{1,0:T(8,128)}), f32[2048,256]{1,0:T(8,128)}) %all-reduce.4.cloned.1.call-update) | async-done | bytes 2097168 | tf_op jit(solution)/shard_map/psum | solution.py:22
  160.2 6.5 %fusion.16 = f32[256,256]{0,1:T(8,128)} fusion(f32[2048,256]{1,0:T(8,128)} %all-reduce.4.cloned.1.call-done), kind=kOutput, calls=%fused_computation.42 | convolution fusion | flops 1610612736 | bytes 2359296 | tf_op jit(solution)/shard_map/dot_general | solution.py:23
  166.8 0.6 reduce-scatter.2.cloned.1.call-start
  167.3 17.0 %all-reduce.6.cloned.1.call-done = f32[256,256]{0,1:T(8,128)} async-done(((f32[256,256]{0,1:T(8,128)}), f32[256,256]{0,1:T(8,128)}) %all-reduce.6.cloned.1.call-update) | async-done | bytes 262160 | tf_op jit(solution)/shard_map/psum | solution.py:26
  184.4 1.1 copy.7
  185.5 1.0 fusion.6
  186.5 11.7 %cholesky.50 = f32[128,128]{1,0:T(8,128)S(1)} custom-call(f32[128,128]{1,0:T(8,128)S(1)} %cholesky.118), custom_call_target="Cholesky" | custom-call | tf_op jit(solution)/shard_map/jit(cholesky)/cholesky | solution.py:27
  198.2 9.8 %custom-call.15 = f32[1,128,128]{1,2,0:T(8,128)S(1)} custom-call(f32[1,128,128]{2,1,0:T(8,128)S(1)} %get-tuple-element.24), custom_call_target="InvertDiagBlocksLowerTriangular" | custom-call | tf_op jit(solution)/shard_map/jit(cholesky)/cholesky | solution.py:27
  208.1 0.2 constant_dynamic-update-slice_fusion.1
  208.3 0.3 convolution_subtract_fusion.1
  208.5 11.7 %cholesky.105 = f32[128,128]{1,0:T(8,128)S(1)} custom-call(f32[128,128]{1,0:T(8,128)S(1)} %convolution_subtract_fusion.1), custom_call_target="Cholesky" | custom-call | tf_op jit(solution)/shard_map/jit(cholesky)/cholesky | solution.py:27
  220.3 0.6 compare_reduce_fusion
  222.3 0.1 triangular_solve.57
  222.3 4.2 %while.1 = (s32[]{:T(128)}, f32[256,256]{1,0:T(8,128)S(1)}, s32[2,2]{1,0:T(2,128)S(1)}, f32[2,128,128]{2,1,0:T(8,128)S(1)}, s32[]{:T(128)}) while((s32[]{:T(128)}, f32[256,256]{1,0:T(8,128)S(1)}, s32[2,2]{1,0:T(2,128)S(1)}, f32[2,128,128]{2,1,0:T(8,128)S(1)}, s32[]{:T(128)}) %tuple.27), condition=%wide.while_cond, body=%wide.while_body.sunk | while | flops 2 | bytes 131189 | solution.py:28
  222.5 0.6 fusion.26
  223.1 1.4 bitcast_dynamic-update-slice_fusion.2
  224.5 0.6 fusion.26
  225.1 1.4 bitcast_dynamic-update-slice_fusion.2
  226.5 19.7 %custom-call.16 = f32[2,128,128]{1,2,0:T(8,128)S(1)} custom-call(f32[2,128,128]{2,1,0:T(8,128)S(1)} %get-tuple-element.10), custom_call_target="InvertDiagBlocksLowerTriangular" | custom-call | tf_op jit(solution)/shard_map/jit(_solve_triangular)/triangular_solve | solution.py:28
  246.2 1.1 fusion.2
  247.3 1.8 convolution_subtract_fusion
  249.1 1.1 fusion.8
  250.2 16.6 %fusion = f32[1024,256]{1,0:T(8,128)} fusion(f32[2048,1024]{1,0:T(8,128)} %param.4, bf16[2048,1024]{1,0:T(8,128)(2,1)S(1)} %copy-done, f32[128,2048]{1,0:T(8,128)S(1)} %fusion.8, f32[128,2048]{1,0:T(8,128)S(1)} %fusion.2), kind=kOutput, calls=%fused_computation.5 | convolution fusion | flops 6447169536 | bytes 15728640 | tf_op jit(solution)/shard_map/dot_general | solution.py:29
  266.9 9.7 %reduce-scatter.2.cloned.1.call-done = f32[512,256]{1,0:T(8,128)} async-done(((f32[1024,256]{1,0:T(8,128)}), f32[512,256]{1,0:T(8,128)}) %reduce-scatter.2.cloned.1.call-update) | async-done | bytes 524304 | tf_op jit(solution)/shard_map/reduce_scatter | solution.py:32
  276.6 1.1 multiply_reduce_fusion
  277.8 40.8 %psum.23 = f32[256]{0:T(256)S(1)} all-reduce(f32[256]{0:T(256)S(1)} %multiply_reduce_fusion), channel_id=1, replica_groups=mesh['col'=16,'row'=2] {'col','row'}, use_global_device_ids=true, to_apply=%region_8.9 | all-reduce | flops 256 | bytes 2048 | tf_op jit(solution)/shard_map/psum | solution.py:33
  318.6 1.9 broadcast_divide_fusion
  320.5 16.1 %multiply_convert_fusion = bf16[2048,1024]{1,0:T(8,128)(2,1)} fusion(f32[128,2048]{1,0:T(8,128)S(1)} %fusion.8, f32[128,2048]{1,0:T(8,128)S(1)} %fusion.2, f32[1024,256]{1,0:T(8,128)} %all-gather.5.cloned.1.call-done, f32[256]{0:T(256)S(1)} %add_sqrt_fusion), kind=kOutput, calls=%fused_computation.2 | convolution fusion | flops 6447431680 | bytes 7341056 | tf_op jit(solution)/shard_map/dot_general | solution.py:44
  336.6 18.4 %multiply_subtract_fusion = f32[2048,1024]{1,0:T(8,128)} fusion(f32[1024,256]{1,0:T(8,128)S(1)} %copy-done.3, f32[2048,1024]{1,0:T(8,128)} %param.4, bf16[2048,1024]{1,0:T(8,128)(2,1)S(1)} %copy-done.1, f32[128,2048]{1,0:T(8,128)S(1)} %fusion.8, f32[128,2048]{1,0:T(8,128)S(1)} %fusion.2), kind=kOutput, calls=%fused_computation.3 | convolution fusion | flops 6451363840 | bytes 24117248 | tf_op jit(solution)/shard_map/dot_general | solution.py:39
  (27 shorter events, 0.4 us)
Async XLA Ops:
  7.2 14.1 %all-gather.3.cloned.1.call-start = ((), (), s32[]{:S(2)}) async-start(), calls=%async_computation.1 | async-start | bytes 1572864 | tf_op jit(solution)/shard_map/all_gather | solution.py:17
  7.9 152.3 %all-reduce.4.cloned.1.call-start = ((), (), s32[]{:S(2)}) async-start(), calls=%async_computation.2 | async-start | bytes 4194304 | tf_op jit(solution)/shard_map/psum | solution.py:22
  32.3 152.1 %all-reduce.6.cloned.1.call-start = ((), (), s32[]{:S(2)}) async-start(), calls=%async_computation.3 | async-start | bytes 524288 | tf_op jit(solution)/shard_map/psum | solution.py:26
  160.2 86.0 %copy-start.2 = (f32[2048,256]{1,0:T(8,128)S(1)}, f32[2048,256]{1,0:T(8,128)}, u32[]{:S(2)}) copy-start(f32[2048,256]{1,0:T(8,128)} %all-reduce.4.cloned.1.call-done) | copy-start | bytes 6291460
  166.8 109.9 %reduce-scatter.2.cloned.1.call-start = ((), (), s32[]{:S(2)}) async-start(), calls=%async_computation.4 | async-start | bytes 1572864 | tf_op jit(solution)/shard_map/reduce_scatter | solution.py:32
  246.2 4.0 %copy-start = (bf16[2048,1024]{1,0:T(8,128)(2,1)S(1)}, bf16[2048,1024]{1,0:T(8,128)(2,1)}, u32[]{:S(2)}) copy-start(bf16[2048,1024]{1,0:T(8,128)(2,1)} %param.3) | copy-start | bytes 12582916
  266.9 53.6 %all-gather.5.cloned.1.call-start = ((), (), s32[]{:S(2)}) async-start(), calls=%async_computation.5 | async-start | bytes 1572864 | tf_op jit(solution)/shard_map/all_gather | solution.py:36
  320.5 16.1 %copy-start.1 = (bf16[2048,1024]{1,0:T(8,128)(2,1)S(1)}, bf16[2048,1024]{1,0:T(8,128)(2,1)}, u32[]{:S(2)}) copy-start(bf16[2048,1024]{1,0:T(8,128)(2,1)} %param.3) | copy-start | bytes 12582916
  320.5 16.1 %copy-start.3 = (f32[1024,256]{1,0:T(8,128)S(1)}, f32[1024,256]{1,0:T(8,128)}, u32[]{:S(2)}) copy-start(f32[1024,256]{1,0:T(8,128)} %all-gather.5.cloned.1.call-done) | copy-start | bytes 3145732
Sparse Core Ops, SparseCore 0:
  9.5 11.7 all-gather.2
  32.4 127.7 all-reduce.3
  166.9 17.4 all-reduce.5
  267.0 9.5 reduce-scatter.1
  278.0 10.2 all-gather.4
where the time goes:
time: 368 us; the launch traced here: 362 us
  waiting for transfers between devices  169 us (46%)
  matrix products  73.1 us (20%)
  other arithmetic  57.7 us (16%)
  blocking collectives  40.8 us (11%)
  between operations  15.5 us (4%)
  local copies, waits for them, and re-layouts  5.14 us (1%)
    psum x1, waiting for transfers between devices, body(): left = lax.psum(partial_value, 'col')  128 us
    psum x1, blocking collectives, body(): squares_right = lax.psum(jnp.sum(share * share, axis=0), ('col', 'row'))  40.8 us
    another operation x6, other arithmetic, body(): lower = jnp.linalg.cholesky(gram)  34 us
    another operation x3, other arithmetic, body(): left_orth = jax.scipy.linalg.solve_triangular(lower, left.T, lower=True).T  19.7 us
    dot_general x1, matrix products, body(): lax.dot_general(left_orth, right_whole, contract_cols, precision=highest,...  18.4 us
    psum x1, waiting for transfers between devices, body(): gram = lax.psum(local_gram, 'row')  17 us
    dot_general x1, matrix products, body(): lax.dot_general(blend, left_orth, contract_rows, precision=highest, prefe...  16.6 us
    dot_general x1, matrix products, body(): lax.dot_general(left_orth, right_unit, contract_cols, precision=highest,...  16.1 us
  transfers between devices with their start and end apart: 5, of which 4 were waited for; matrix products, arithmetic and copies ran while one was open for 1% of the time, Pallas kernels for 0%

commit v1 on v0

--- a/solution.py
+++ b/solution.py
@@ -30,7 +30,8 @@
         blend, left_orth, contract_rows, precision=highest, preferred_element_type=jnp.float32
     )
     share = lax.psum_scatter(right_local, "row", scatter_dimension=0, tiled=True)
-    squares_right = lax.psum(jnp.sum(share * share, axis=0), ("col", "row"))
+    _update_sites = lambda packet: lax.psum(lax.psum(packet, "row"), axis_name="col")
+    squares_right = _update_sites(jnp.sum(share * share, axis=0))
     right_norm = jnp.sqrt(squares_right + EPS)
     right_next = share / right_norm[None, :]
     right_whole = lax.all_gather(share, "row", axis=0, tiled=True)

time: 368 us -> 372 us (1.011)
  blocking collectives: 40.8 us -> 44.7 us
    psum x1 -> x2, blocking collectives: 40.8 us -> 44.7 us  [the longest x1 42.2 us: body(): lax.psum(lax.psum(packet, 'row'), axis_name='col')]
where the time goes in v1:
time: 372 us; the launch traced here: 366 us
  waiting for transfers between devices  169 us (45%)
  matrix products  73.1 us (20%)
  other arithmetic  57.7 us (16%)
  blocking collectives  44.7 us (12%)
  between operations  15.5 us (4%)
  local copies, waits for them, and re-layouts  5.14 us (1%)
    psum x1, waiting for transfers between devices, body(): left = lax.psum(partial_value, 'col')  128 us
    psum x1, blocking collectives, body(): lax.psum(lax.psum(packet, 'row'), axis_name='col')  42.2 us
    another operation x6, other arithmetic, body(): lower = jnp.linalg.cholesky(gram)  34 us
    another operation x3, other arithmetic, body(): left_orth = jax.scipy.linalg.solve_triangular(lower, left.T, lower=True).T  19.7 us
    dot_general x1, matrix products, body(): lax.dot_general(left_orth, right_whole, contract_cols, precision=highest,...  18.4 us
    psum x1, waiting for transfers between devices, body(): gram = lax.psum(local_gram, 'row')  17 us
    dot_general x1, matrix products, body(): lax.dot_general(blend, left_orth, contract_rows, precision=highest, prefe...  16.6 us
    dot_general x1, matrix products, body(): lax.dot_general(left_orth, right_unit, contract_cols, precision=highest,...  16.1 us
  transfers between devices with their start and end apart: 5, of which 4 were waited for; matrix products, arithmetic and copies ran while one was open for 1% of the time, Pallas kernels for 0%

profile of v1, /device:TPU:0, one launch (start us, length us, event | category | flops | bytes accessed | tf_op | source)
XLA Modules:
  0.0 365.7 jit_solution(13230017484694093963)
XLA Ops:
  7.2 0.7 all-gather.3.cloned.1.call-update
  7.9 13.4 %all-gather.3.cloned.1.call-done = f32[1024,256]{1,0:T(8,128)} async-done(((f32[512,256]{1,0:T(8,128)}), f32[1024,256]{1,0:T(8,128)}) %all-gather.3.cloned.1.call-update) | async-done | bytes 1048592 | tf_op jit(solution)/shard_map/all_gather | solution.py:17
  21.3 11.0 %fusion.1 = f32[2048,256]{1,0:T(8,128)} fusion(f32[1024,256]{1,0:T(8,128)} %all-gather.3.cloned.1.call-done, f32[2048,1024]{1,0:T(8,128)} %param.4, bf16[2048,1024]{1,0:T(8,128)(2,1)} %param.3), kind=kOutput, calls=%fused_computation.6 | convolution fusion | flops 6446645248 | bytes 15728640 | tf_op jit(solution)/shard_map/dot_general | solution.py:19
  32.3 127.9 %all-reduce.4.cloned.1.call-done = f32[2048,256]{1,0:T(8,128)} async-done(((f32[2048,256]{1,0:T(8,128)}), f32[2048,256]{1,0:T(8,128)}) %all-reduce.4.cloned.1.call-update) | async-done | bytes 2097168 | tf_op jit(solution)/shard_map/psum | solution.py:22
  160.2 6.5 %fusion.16 = f32[256,256]{0,1:T(8,128)} fusion(f32[2048,256]{1,0:T(8,128)} %all-reduce.4.cloned.1.call-done), kind=kOutput, calls=%fused_computation.42 | convolution fusion | flops 1610612736 | bytes 2359296 | tf_op jit(solution)/shard_map/dot_general | solution.py:23
  166.8 0.6 reduce-scatter.2.cloned.1.call-start
  167.3 17.0 %all-reduce.6.cloned.1.call-done = f32[256,256]{0,1:T(8,128)} async-done(((f32[256,256]{0,1:T(8,128)}), f32[256,256]{0,1:T(8,128)}) %all-reduce.6.cloned.1.call-update) | async-done | bytes 262160 | tf_op jit(solution)/shard_map/psum | solution.py:26
  184.4 1.1 copy.7
  185.5 1.0 fusion.6
  186.5 11.7 %cholesky.50 = f32[128,128]{1,0:T(8,128)S(1)} custom-call(f32[128,128]{1,0:T(8,128)S(1)} %cholesky.118), custom_call_target="Cholesky" | custom-call | tf_op jit(solution)/shard_map/jit(cholesky)/cholesky | solution.py:27
  198.2 9.8 %custom-call.15 = f32[1,128,128]{1,2,0:T(8,128)S(1)} custom-call(f32[1,128,128]{2,1,0:T(8,128)S(1)} %get-tuple-element.24), custom_call_target="InvertDiagBlocksLowerTriangular" | custom-call | tf_op jit(solution)/shard_map/jit(cholesky)/cholesky | solution.py:27
  208.1 0.2 constant_dynamic-update-slice_fusion.1
  208.3 0.3 convolution_subtract_fusion.1
  208.5 11.7 %cholesky.105 = f32[128,128]{1,0:T(8,128)S(1)} custom-call(f32[128,128]{1,0:T(8,128)S(1)} %convolution_subtract_fusion.1), custom_call_target="Cholesky" | custom-call | tf_op jit(solution)/shard_map/jit(cholesky)/cholesky | solution.py:27
  220.3 0.6 compare_reduce_fusion
  222.3 4.2 %while.1 = (s32[]{:T(128)}, f32[256,256]{1,0:T(8,128)S(1)}, s32[2,2]{1,0:T(2,128)S(1)}, f32[2,128,128]{2,1,0:T(8,128)S(1)}, s32[]{:T(128)}) while((s32[]{:T(128)}, f32[256,256]{1,0:T(8,128)S(1)}, s32[2,2]{1,0:T(2,128)S(1)}, f32[2,128,128]{2,1,0:T(8,128)S(1)}, s32[]{:T(128)}) %tuple.27), condition=%wide.while_cond, body=%wide.while_body.sunk | while | flops 2 | bytes 131189 | solution.py:28
  222.5 0.6 fusion.26
  223.1 1.4 bitcast_dynamic-update-slice_fusion.2
  224.5 0.6 fusion.26
  225.1 1.4 bitcast_dynamic-update-slice_fusion.2
  226.5 19.7 %custom-call.16 = f32[2,128,128]{1,2,0:T(8,128)S(1)} custom-call(f32[2,128,128]{2,1,0:T(8,128)S(1)} %get-tuple-element.10), custom_call_target="InvertDiagBlocksLowerTriangular" | custom-call | tf_op jit(solution)/shard_map/jit(_solve_triangular)/triangular_solve | solution.py:28
  246.2 1.1 fusion.2
  247.3 1.8 convolution_subtract_fusion
  249.1 1.1 fusion.8
  250.2 16.6 %fusion = f32[1024,256]{1,0:T(8,128)} fusion(f32[2048,1024]{1,0:T(8,128)} %param.4, bf16[2048,1024]{1,0:T(8,128)(2,1)S(1)} %copy-done, f32[128,2048]{1,0:T(8,128)S(1)} %fusion.8, f32[128,2048]{1,0:T(8,128)S(1)} %fusion.2), kind=kOutput, calls=%fused_computation.5 | convolution fusion | flops 6447169536 | bytes 15728640 | tf_op jit(solution)/shard_map/dot_general | solution.py:29
  266.9 9.7 %reduce-scatter.2.cloned.1.call-done = f32[512,256]{1,0:T(8,128)} async-done(((f32[1024,256]{1,0:T(8,128)}), f32[512,256]{1,0:T(8,128)}) %reduce-scatter.2.cloned.1.call-update) | async-done | bytes 524304 | tf_op jit(solution)/shard_map/reduce_scatter | solution.py:32
  276.6 1.1 multiply_reduce_fusion
  277.8 2.5 psum.30
  280.2 42.2 %psum.31 = f32[256]{0:T(256)S(1)} all-reduce(f32[256]{0:T(256)S(1)} %psum.30), channel_id=1, replica_groups=mesh['col'=16,'row'=2] {'col'}, use_global_device_ids=true, to_apply=%region_9.10 | all-reduce | flops 256 | bytes 2048 | tf_op jit(solution)/shard_map/psum | solution.py:33
  322.5 1.9 broadcast_divide_fusion
  324.3 16.1 %multiply_convert_fusion = bf16[2048,1024]{1,0:T(8,128)(2,1)} fusion(f32[128,2048]{1,0:T(8,128)S(1)} %fusion.8, f32[128,2048]{1,0:T(8,128)S(1)} %fusion.2, f32[1024,256]{1,0:T(8,128)} %all-gather.5.cloned.1.call-done, f32[256]{0:T(256)S(1)} %add_sqrt_fusion), kind=kOutput, calls=%fused_computation.2 | convolution fusion | flops 6447431680 | bytes 7341056 | tf_op jit(solution)/shard_map/dot_general | solution.py:45
  340.5 18.4 %multiply_subtract_fusion = f32[2048,1024]{1,0:T(8,128)} fusion(f32[1024,256]{1,0:T(8,128)S(1)} %copy-done.3, f32[2048,1024]{1,0:T(8,128)} %param.4, bf16[2048,1024]{1,0:T(8,128)(2,1)S(1)} %copy-done.1, f32[128,2048]{1,0:T(8,128)S(1)} %fusion.8, f32[128,2048]{1,0:T(8,128)S(1)} %fusion.2), kind=kOutput, calls=%fused_computation.3 | convolution fusion | flops 6451363840 | bytes 24117248 | tf_op jit(solution)/shard_map/dot_general | solution.py:40
  (28 shorter events, 0.5 us)
Async XLA Ops:
  7.2 14.1 %all-gather.3.cloned.1.call-start = ((), (), s32[]{:S(2)}) async-start(), calls=%async_computation.1 | async-start | bytes 1572864 | tf_op jit(solution)/shard_map/all_gather | solution.py:17
  7.9 152.3 %all-reduce.4.cloned.1.call-start = ((), (), s32[]{:S(2)}) async-start(), calls=%async_computation.2 | async-start | bytes 4194304 | tf_op jit(solution)/shard_map/psum | solution.py:22
  32.3 152.1 %all-reduce.6.cloned.1.call-start = ((), (), s32[]{:S(2)}) async-start(), calls=%async_computation.3 | async-start | bytes 524288 | tf_op jit(solution)/shard_map/psum | solution.py:26
  160.2 86.0 %copy-start.2 = (f32[2048,256]{1,0:T(8,128)S(1)}, f32[2048,256]{1,0:T(8,128)}, u32[]{:S(2)}) copy-start(f32[2048,256]{1,0:T(8,128)} %all-reduce.4.cloned.1.call-done) | copy-start | bytes 6291460
  166.8 109.9 %reduce-scatter.2.cloned.1.call-start = ((), (), s32[]{:S(2)}) async-start(), calls=%async_computation.4 | async-start | bytes 1572864 | tf_op jit(solution)/shard_map/reduce_scatter | solution.py:32
  246.2 4.0 %copy-start = (bf16[2048,1024]{1,0:T(8,128)(2,1)S(1)}, bf16[2048,1024]{1,0:T(8,128)(2,1)}, u32[]{:S(2)}) copy-start(bf16[2048,1024]{1,0:T(8,128)(2,1)} %param.3) | copy-start | bytes 12582916
  266.9 57.5 %all-gather.5.cloned.1.call-start = ((), (), s32[]{:S(2)}) async-start(), calls=%async_computation.5 | async-start | bytes 1572864 | tf_op jit(solution)/shard_map/all_gather | solution.py:37
  324.3 16.1 %copy-start.1 = (bf16[2048,1024]{1,0:T(8,128)(2,1)S(1)}, bf16[2048,1024]{1,0:T(8,128)(2,1)}, u32[]{:S(2)}) copy-start(bf16[2048,1024]{1,0:T(8,128)(2,1)} %param.3) | copy-start | bytes 12582916
  324.3 16.1 %copy-start.3 = (f32[1024,256]{1,0:T(8,128)S(1)}, f32[1024,256]{1,0:T(8,128)}, u32[]{:S(2)}) copy-start(f32[1024,256]{1,0:T(8,128)} %all-gather.5.cloned.1.call-done) | copy-start | bytes 3145732
Sparse Core Ops, SparseCore 0:
  9.5 11.7 all-gather.2
  32.4 127.7 all-reduce.3
  166.9 17.4 all-reduce.5
  267.0 9.5 reduce-scatter.1
  278.0 10.2 all-gather.4
